TPU v7x, 32 devices: a whole 2x2x4 slice. The times are simulated.
32 devices in a mesh: rep: 8 (over z, y), shard: 4 (over x, core).
Axes of the slice: x: 2, y: 2, z: 4, core: 2. Of those that a mesh axis runs over, the one named last changes fastest.
Arguments:
- activ: bfloat16 [4096, 8192], P(('rep', 'shard')), may hold values from -6 to 6
- key_grad: bfloat16 [4096, 640], P(('rep', 'shard')), may hold values from -1.1953125 to 1.1953125
- key_weight: bfloat16 [8192, 640], P('shard'), may hold values from -0.25 to 0.25
- feedback: bfloat16 [8, 40960, 128], P('rep', 'shard'), may hold values from -24 to 24
- kept: int32 [8, 4, 512], P('rep', 'shard'), may hold values from 0 to 10239, as said below
- region_len: int32 [4, 8], P('shard'), may hold values from 640 to 1920, as said below
Outputs:
- input_grad: bfloat16 [4096, 8192], P(('rep', 'shard'))
- next_feedback: bfloat16 [8, 40960, 128], P('rep', 'shard')
- owned_sum: float32 [4, 15360, 128], P('shard', 'rep')
Inputs may be any that keep to these rules, and one draw needn't show every extreme that they name: `region_len`: each row splits its shard's 10240 blocks into 8 regions in order of owner and sums to 10240; every row has a region of exactly 1920 blocks. `kept`: the 512 numbers of a row are different blocks of that shard. At most 128 of them lie in one region of the shard; every row has exactly 128 in some region, and in every shard some region gets exactly 128 from every replica.
All inputs are finite; a program needn't handle non-finite values.
Results may differ from a plain program's by a relative error of at most 0.011.
Values may be sent and summed in bfloat16 or wider, within the bound.
A program may use at most 128 MiB of HBM per device.

v0:
```python
import jax
import jax.numpy as jnp
from jax import lax
from jax.sharding import PartitionSpec as P


def accumulate(block_rows, block_ids, own_start, own_len, region_max):
    offset = block_ids - own_start
    inside = (offset >= 0) & (offset < own_len)
    target = jnp.where(inside, offset, region_max)
    blank = jnp.zeros((region_max, block_rows.shape[1]), jnp.float32)
    return blank.at[target].add(block_rows.astype(jnp.float32), mode="drop")


def per_device(activ, key_grad, key_weight, feedback, kept, region_len):
    grads_all = lax.all_gather(key_grad, "shard", axis=0, tiled=True)
    act_cols = lax.all_to_all(activ, "shard", split_axis=1, concat_axis=0, tiled=True)
    weight_grad = lax.dot_general(
        act_cols, grads_all, (((0,), (0,)), ((), ())), preferred_element_type=jnp.float32
    )
    input_cols = lax.dot_general(
        grads_all, key_weight, (((1,), (1,)), ((), ())), preferred_element_type=jnp.float32
    ).astype(jnp.bfloat16)
    input_grad = lax.all_to_all(input_cols, "shard", split_axis=0, concat_axis=1, tiled=True)
    table = feedback[0]
    chosen = kept[0, 0]
    lengths = region_len[0]
    replicas = lax.axis_size("rep")
    block_count = table.shape[0]
    block_size = table.shape[1]
    keep_count = chosen.shape[0]
    mean_len = block_count // replicas
    region_max = mean_len + mean_len // 2
    starts = jnp.cumsum(lengths) - lengths
    owner_self = lax.axis_index("rep")
    own_start = starts[owner_self]
    own_len = lengths[owner_self]
    kept_rows = table[chosen]
    flags = jnp.zeros((block_count,), bool).at[chosen].set(True)
    cleared = jnp.where(flags[:, None], jnp.float32(0.0), table.astype(jnp.float32))
    next_feedback = (cleared + weight_grad.reshape(block_count, block_size)).astype(jnp.bfloat16)[
        None
    ]
    owner_id = jnp.sum((starts[None, :] <= chosen[:, None]).astype(jnp.int32), axis=1) - 1
    serial = jnp.arange(keep_count, dtype=jnp.int32)
    earlier = (owner_id[:, None] == owner_id[None, :]) & (serial[None, :] < serial[:, None])
    slot_index = jnp.sum(earlier.astype(jnp.int32), axis=1)
    capacity = 2 * keep_count // replicas
    place_at = owner_id * capacity + slot_index
    send_rows = (
        jnp.zeros((replicas * capacity, block_size), jnp.bfloat16).at[place_at].set(kept_rows)
    )
    send_ids = jnp.full((replicas * capacity,), -1, jnp.int32).at[place_at].set(chosen)
    got_rows, got_ids = (
        lax.all_to_all(send_rows, "rep", split_axis=0, concat_axis=0, tiled=True),
        lax.all_to_all(send_ids, "rep", split_axis=0, concat_axis=0, tiled=True),
    )
    owned_rows = accumulate(got_rows, got_ids, own_start, own_len, region_max)
    return (input_grad, next_feedback, owned_rows[None])


def solution(mesh):
    return jax.shard_map(
        per_device,
        mesh=mesh,
        in_specs=(
            P(("rep", "shard"), None),
            P(("rep", "shard"), None),
            P("shard", None),
            P("rep", "shard", None),
            P("rep", "shard", None),
            P("shard", None),
        ),
        out_specs=(P(("rep", "shard"), None), P("rep", "shard", None), P("shard", "rep", None)),
        check_vma=False,
    )
```

profile of v0, /device:TPU:0, one launch (start us, length us, event | category | flops | bytes accessed | tf_op | source)
XLA Modules:
  0.0 117.7 jit_solution(1622688939139694994)
XLA Ops:
  0.6 0.0 copy-start
  0.6 1.0 reduce-window.4
  1.6 0.7 fusion.11
  2.3 0.8 convert_reduce_fusion.1
  3.1 0.3 convert_reduce_fusion
  3.3 3.2 %scatter_custom_fusion.1 = s32[1024]{0:T(1024)} fusion(s32[512]{0:T(512)S(1)} %bitcast.56, s32[512]{0:T(512)} %bitcast.54, s32[]{:T(128)} %constant.18.clone.1), kind=kCustom, calls=%fused_computation.26 | custom fusion | bytes 4608 | tf_op jit(solution)/shard_map/scatter | solution.py:53
  6.5 7.3 %all-to-all-start.2 = ((s32[8,128,1]{1,2,0:T(1,128)}), s32[8,128,1]{1,2,0:T(1,128)S(1)}, u32[]{:S(2)}, u32[]{:S(2)}) async-start(s32[8,128,1]{1,2,0:T(1,128)} %bitcast.14), calls=%async_computation.2 | async-start | bytes 8192 | tf_op jit(solution)/shard_map/all_to_all | solution.py:56
  13.8 0.7 compare_select_fusion.2
  14.5 0.0 copy-start.2
  14.5 0.6 copy-done.2
  15.1 5.5 %scatter_custom_fusion.2 = bf16[1024,128]{1,0:T(8,128)(2,1)} fusion(s32[512]{0:T(512)S(1)} %bitcast.57, bf16[]{:T(256)} %constant.12.clone.1, bf16[10240,128]{1,0:T(8,128)(2,1)} %bitcast.43, s32[1024]{0:T(1024)S(1)} %pad_clamp_fusion), kind=kCustom, calls=%fused_computation.13 | custom fusion | bytes 262656 | tf_op jit(solution)/shard_map/scatter | solution.py:51
  20.6 0.0 all-to-all-done.2
  20.6 6.0 %all-to-all-start.3 = ((bf16[8,128,128]{2,1,0:T(8,128)(2,1)}), bf16[8,128,128]{2,1,0:T(8,128)(2,1)S(1)}, u32[]{:S(2)}, u32[]{:S(2)}) async-start(bf16[8,128,128]{2,1,0:T(8,128)(2,1)} %bitcast.23), calls=%async_computation.3 | async-start | bytes 524288 | tf_op jit(solution)/shard_map/all_to_all | solution.py:55
  26.6 4.1 %copy.20 = bf16[128,8192]{0,1:T(8,128)(2,1)} copy(bf16[128,8192]{1,0:T(8,128)(2,1)} %param.6) | data formatting | bytes 4194304 | tf_op args[0]
  30.7 4.4 %all-to-all-done.3 = bf16[8,128,128]{2,1,0:T(8,128)(2,1)S(1)} async-done(((bf16[8,128,128]{2,1,0:T(8,128)(2,1)}), bf16[8,128,128]{2,1,0:T(8,128)(2,1)S(1)}, u32[]{:S(2)}, u32[]{:S(2)}) %all-to-all-start.3) | async-done | bytes 262176 | tf_op jit(solution)/shard_map/all_to_all | solution.py:55
  35.1 4.4 %all-to-all-start.1 = ((bf16[128,4,2048]{0,2,1:T(8,128)(2,1)}), bf16[128,4,2048]{0,2,1:T(8,128)(2,1)}, u32[]{:S(2)}, u32[]{:S(2)}) async-start(bf16[128,4,2048]{0,2,1:T(8,128)(2,1)} %bitcast.42), calls=%async_computation.1 | async-start | bytes 4194304 | tf_op jit(solution)/shard_map/all_to_all | solution.py:17
  39.6 30.0 %all_gather.3 = bf16[512,640]{1,0:T(8,128)(2,1)S(1)} all-gather(bf16[128,640]{1,0:T(8,128)(2,1)} %param.7), channel_id=1, replica_groups=mesh['rep'=8,'shard'=4] {'shard'}, dimensions={0}, use_global_device_ids=true | all-gather | bytes 819200 | tf_op jit(solution)/shard_map/all_gather | solution.py:16
  69.6 0.0 copy-done
  69.6 3.1 %convolution_convert_fusion = bf16[512,2048]{1,0:T(8,128)(2,1)} fusion(bf16[512,640]{1,0:T(8,128)(2,1)S(1)} %all_gather.3, bf16[2048,640]{1,0:T(8,128)(2,1)S(1)} %copy-done), kind=kOutput, calls=%fused_computation.6 | convolution fusion | flops 1343225856 | bytes 5373952 | tf_op jit(solution)/shard_map/dot_general | solution.py:21
  72.7 0.0 copy-start.3
  72.7 0.0 all-to-all-done.1
  72.7 4.6 %all-to-all-start = ((bf16[4,128,2048]{2,1,0:T(8,128)(2,1)}), bf16[4,128,2048]{2,1,0:T(8,128)(2,1)}, u32[]{:S(2)}, u32[]{:S(2)}) async-start(bf16[4,128,2048]{2,1,0:T(8,128)(2,1)} %bitcast.44), calls=%async_computation | async-start | bytes 4194304 | tf_op jit(solution)/shard_map/all_to_all | solution.py:24
  77.4 0.0 copy-done.3
  77.4 0.6 constant_dynamic-slice_fusion
  78.0 0.6 dynamic_slice.6
  78.6 0.5 broadcast.121
  79.1 2.6 %scatter_custom_fusion = pred[10240]{0:T(1024)(128)(4,1)S(1)} fusion(s32[512]{0:T(512)} %bitcast.51, pred[512]{0:T(512)(128)(4,1)} %broadcast.121, pred[]{:T(512)} %constant.13.clone.1), kind=kCustom, calls=%fused_computation.17 | custom fusion | bytes 10752 | tf_op jit(solution)/shard_map/scatter | solution.py:39
  81.7 0.7 broadcast_subtract_fusion
  82.3 0.6 compare_select_fusion
  83.0 7.0 %scatter_custom_fusion.3 = f32[1920,128]{1,0:T(8,128)} fusion(s32[1024]{0:T(1024)S(1)} %bitcast.55, bf16[1024,128]{1,0:T(8,128)(2,1)S(1)} %bitcast.46, f32[]{:T(128)} %constant.17.clone.1), kind=kCustom, calls=%fused_computation.10 | custom fusion | flops 262144 | bytes 1245188 | tf_op jit(solution)/shard_map/scatter-add | solution.py:12
  90.0 3.9 %copy.21 = bf16[4,128,2048]{2,1,0:T(8,128)(2,1)} copy(bf16[4,128,2048]{1,2,0:T(8,128)(2,1)} %bitcast.5) | data formatting | bytes 4194304 | tf_op jit(solution)/shard_map/all_to_all | solution.py:17
  93.9 5.8 %fusion.12 = f32[2048,640]{1,0:T(8,128)} fusion(bf16[512,2048]{1,0:T(8,128)(2,1)} %bitcast.41, bf16[512,640]{1,0:T(8,128)(2,1)S(1)} %all_gather.3), kind=kOutput, calls=%fused_computation.33 | convolution fusion | flops 1342177280 | bytes 7995392 | tf_op jit(solution)/shard_map/dot_general | solution.py:18
  99.7 6.5 %reshape.138 = f32[1,10240,128]{2,1,0:T(8,128)} reshape(f32[2048,640]{1,0:T(8,128)} %fusion.12) | data formatting | bytes 10485760 | tf_op jit(solution)/shard_map/reshape | solution.py:41
  106.2 0.0 all-to-all-done
  106.2 0.0 copy-start.1
  106.2 3.3 %copy.24 = bf16[4,16,8,2048]{3,2,0,1:T(8,128)(2,1)} copy(bf16[4,16,8,2048]{3,2,1,0:T(8,128)(2,1)} %bitcast.28) | data formatting | bytes 4194304 | tf_op jit(solution)/shard_map/all_to_all | solution.py:24
  109.5 0.0 copy-done.1
  109.5 8.2 %add_convert_fusion = bf16[1,10240,128]{2,1,0:T(8,128)(2,1)} fusion(f32[1,10240,128]{2,1,0:T(8,128)} %reshape.138, bf16[1,10240,128]{2,1,0:T(8,128)(2,1)S(1)} %copy-done.1, pred[10240]{0:T(1024)(128)(4,1)S(1)} %scatter_custom_fusion), kind=kLoop, calls=%fused_computation.5 | loop fusion | flops 5242880 | bytes 10496000 | tf_op jit(solution)/shard_map/convert_element_type | solution.py:41
  (5 shorter events, 0.0 us)
Async XLA Ops:
  0.6 68.9 %copy-start = (bf16[2048,640]{1,0:T(8,128)(2,1)S(1)}, bf16[2048,640]{1,0:T(8,128)(2,1)}, u32[]{:S(2)}) copy-start(bf16[2048,640]{1,0:T(8,128)(2,1)} %param.8) | copy-start | bytes 7864324
  6.5 14.1 %all-to-all-start.2 = ((s32[8,128,1]{1,2,0:T(1,128)}), s32[8,128,1]{1,2,0:T(1,128)S(1)}, u32[]{:S(2)}, u32[]{:S(2)}) async-start(s32[8,128,1]{1,2,0:T(1,128)} %bitcast.14), calls=%async_computation.2 | async-start | bytes 8192 | tf_op jit(solution)/shard_map/all_to_all | solution.py:56
  14.5 0.6 copy-start.2
  20.6 14.5 %all-to-all-start.3 = ((bf16[8,128,128]{2,1,0:T(8,128)(2,1)}), bf16[8,128,128]{2,1,0:T(8,128)(2,1)S(1)}, u32[]{:S(2)}, u32[]{:S(2)}) async-start(bf16[8,128,128]{2,1,0:T(8,128)(2,1)} %bitcast.23), calls=%async_computation.3 | async-start | bytes 524288 | tf_op jit(solution)/shard_map/all_to_all | solution.py:55
  35.1 37.6 %all-to-all-start.1 = ((bf16[128,4,2048]{0,2,1:T(8,128)(2,1)}), bf16[128,4,2048]{0,2,1:T(8,128)(2,1)}, u32[]{:S(2)}, u32[]{:S(2)}) async-start(bf16[128,4,2048]{0,2,1:T(8,128)(2,1)} %bitcast.42), calls=%async_computation.1 | async-start | bytes 4194304 | tf_op jit(solution)/shard_map/all_to_all | solution.py:17
  72.7 4.6 %copy-start.3 = (s32[1,8]{1,0:T(1,128)S(1)}, s32[1,8]{1,0:T(1,128)}, u32[]{:S(2)}) copy-start(s32[1,8]{1,0:T(1,128)} %param.11) | copy-start | bytes 100
  72.7 33.5 %all-to-all-start = ((bf16[4,128,2048]{2,1,0:T(8,128)(2,1)}), bf16[4,128,2048]{2,1,0:T(8,128)(2,1)}, u32[]{:S(2)}, u32[]{:S(2)}) async-start(bf16[4,128,2048]{2,1,0:T(8,128)(2,1)} %bitcast.44), calls=%async_computation | async-start | bytes 4194304 | tf_op jit(solution)/shard_map/all_to_all | solution.py:24
  106.2 3.3 %copy-start.1 = (bf16[1,10240,128]{2,1,0:T(8,128)(2,1)S(1)}, bf16[1,10240,128]{2,1,0:T(8,128)(2,1)}, u32[]{:S(2)}) copy-start(bf16[1,10240,128]{2,1,0:T(8,128)(2,1)} %param.9) | copy-start | bytes 7864324
where the time goes:
time: 119 us; the launch traced here: 118 us
  local copies, waits for them, and re-layouts  31.4 us (26%)
  blocking collectives  30 us (25%)
  starting transfers between devices  22.4 us (19%)
  other arithmetic  19.8 us (17%)
  matrix products  8.92 us (7%)
  waiting for transfers between devices  4.45 us (4%)
    all_gather x1, blocking collectives, per_device(): grads_all = lax.all_gather(key_grad, 'shard', axis=0, tiled=True)  30 us
    convert_element_type x1, other arithmetic, per_device(): (cleared + weight_grad.reshape(block_count, block_size)).astype(jnp.bfloa...  8.16 us
    all_to_all x1, starting transfers between devices, per_device(): lax.all_to_all(send_ids, 'rep', split_axis=0, concat_axis=0, tiled=True)  7.31 us
    scatter-add x1, other arithmetic, accumulate(): return blank.at[target].add(block_rows.astype(jnp.float32), mode='drop')  7.02 us
    reshape x1, local copies, waits for them, and re-layouts, per_device(): weight_grad.reshape(block_count, block_size)  6.47 us
    all_to_all x1, starting transfers between devices, per_device(): lax.all_to_all(send_rows, 'rep', split_axis=0, concat_axis=0, tiled=True)  6 us
    dot_general x1, matrix products, per_device(): lax.dot_general(act_cols, grads_all, (((0,), (0,)), ((), ())), preferred_...  5.78 us
    scatter x1, local copies, waits for them, and re-layouts, per_device(): jnp.zeros((replicas * capacity, block_size), jnp.bfloat16).at[place_at]  5.51 us
  transfers between devices with their start and end apart: 4, of which 1 were waited for; matrix products, arithmetic and copies ran while one was open for 36% of the time, Pallas kernels for 0%

commit v1 on v0

--- a/solution.py
+++ b/solution.py
@@ -14,7 +14,10 @@
 
 def per_device(activ, key_grad, key_weight, feedback, kept, region_len):
     grads_all = lax.all_gather(key_grad, "shard", axis=0, tiled=True)
-    act_cols = lax.all_to_all(activ, "shard", split_axis=1, concat_axis=0, tiled=True)
+    act_cols = jnp.concatenate(
+        lax.all_to_all(jnp.stack(jnp.split(activ, lax.axis_size("shard"), axis=1)), "shard", 0, 0),
+        axis=0,
+    )
     weight_grad = lax.dot_general(
         act_cols, grads_all, (((0,), (0,)), ((), ())), preferred_element_type=jnp.float32
     )

time: 119 us -> 116 us (0.975)
  local copies, waits for them, and re-layouts: 31.4 us -> 25 us
  waiting for transfers between devices: 4.45 us -> 6.2 us
  other arithmetic: 19.8 us -> 21.4 us
    unnamed x9 -> x8, local copies, waits for them, and re-layouts: 4.68 us -> 0.61 us
    all_to_all x1 -> x0, local copies, waits for them, and re-layouts: 3.94 us -> none  [per_device(): lax.all_to_all(activ, 'shard', split_axis=1, concat_axis=0, tiled=True)]
    another operation x0 -> x1, local copies, waits for them, and re-layouts: none -> 1.65 us  [per_device(): jnp.stack(jnp.split(activ, lax.axis_size('shard'), axis=1))]
    another operation x1 -> x2, other arithmetic: 0.98 us -> 2.56 us  [the longest x1 1.58 us: per_device(): jnp.stack(jnp.split(activ, lax.axis_size('shard'), axis=1))]
  transfers between devices with their start and end apart: 4 -> 4, of which waited for: 1 -> 2; matrix products, arithmetic and copies ran while one was open for 36% -> 33% of each run, Pallas kernels for 0% -> 0%
where the time goes in v1:
time: 116 us; the launch traced here: 115 us
  blocking collectives  30 us (26%)
  local copies, waits for them, and re-layouts  25 us (22%)
  starting transfers between devices  22.4 us (19%)
  other arithmetic  21.4 us (18%)
  matrix products  8.88 us (8%)
  waiting for transfers between devices  6.2 us (5%)
    all_gather x1, blocking collectives, per_device(): grads_all = lax.all_gather(key_grad, 'shard', axis=0, tiled=True)  30 us
    convert_element_type x1, other arithmetic, per_device(): (cleared + weight_grad.reshape(block_count, block_size)).astype(jnp.bfloa...  8.16 us
    all_to_all x1, starting transfers between devices, per_device(): lax.all_to_all(send_ids, 'rep', split_axis=0, concat_axis=0, tiled=True)  7.31 us
    scatter-add x1, other arithmetic, accumulate(): return blank.at[target].add(block_rows.astype(jnp.float32), mode='drop')  7.02 us
    reshape x1, local copies, waits for them, and re-layouts, per_device(): weight_grad.reshape(block_count, block_size)  6.48 us
    all_to_all x1, starting transfers between devices, per_device(): lax.all_to_all(send_rows, 'rep', split_axis=0, concat_axis=0, tiled=True)  6 us
    dot_general x1, matrix products, per_device(): lax.dot_general(act_cols, grads_all, (((0,), (0,)), ((), ())), preferred_...  5.73 us
    scatter x1, local copies, waits for them, and re-layouts, per_device(): jnp.zeros((replicas * capacity, block_size), jnp.bfloat16).at[place_at]  5.51 us
  transfers between devices with their start and end apart: 4, of which 2 were waited for; matrix products, arithmetic and copies ran while one was open for 33% of the time, Pallas kernels for 0%

profile of v1, /device:TPU:0, one launch (start us, length us, event | category | flops | bytes accessed | tf_op | source)
XLA Modules:
  0.0 114.6 jit_solution(15284508649840407491)
XLA Ops:
  0.6 0.0 copy-start
  0.6 1.0 reduce-window.4
  1.6 0.7 fusion.11
  2.3 0.8 convert_reduce_fusion.1
  3.1 0.3 convert_reduce_fusion
  3.3 3.2 %scatter_custom_fusion.1 = s32[1024]{0:T(1024)} fusion(s32[512]{0:T(512)S(1)} %bitcast.60, s32[512]{0:T(512)} %bitcast.58, s32[]{:T(128)} %constant.18.clone.1), kind=kCustom, calls=%fused_computation.31 | custom fusion | bytes 4608 | tf_op jit(solution)/shard_map/scatter | solution.py:56
  6.5 7.3 %all-to-all-start.2 = ((s32[8,128,1]{1,2,0:T(1,128)}), s32[8,128,1]{1,2,0:T(1,128)S(1)}, u32[]{:S(2)}, u32[]{:S(2)}) async-start(s32[8,128,1]{1,2,0:T(1,128)} %bitcast.16), calls=%async_computation.2 | async-start | bytes 8192 | tf_op jit(solution)/shard_map/all_to_all | solution.py:59
  13.8 0.7 compare_select_fusion.2
  14.5 0.0 copy-start.2
  14.5 0.6 copy-done.2
  15.1 5.5 %scatter_custom_fusion.2 = bf16[1024,128]{1,0:T(8,128)(2,1)} fusion(s32[512]{0:T(512)S(1)} %bitcast.61, bf16[]{:T(256)} %constant.12.clone.1, bf16[10240,128]{1,0:T(8,128)(2,1)} %bitcast.47, s32[1024]{0:T(1024)S(1)} %pad_clamp_fusion), kind=kCustom, calls=%fused_computation.18 | custom fusion | bytes 262656 | tf_op jit(solution)/shard_map/scatter | solution.py:54
  20.6 0.0 all-to-all-done.2
  20.6 6.0 %all-to-all-start.3 = ((bf16[8,128,128]{2,1,0:T(8,128)(2,1)}), bf16[8,128,128]{2,1,0:T(8,128)(2,1)S(1)}, u32[]{:S(2)}, u32[]{:S(2)}) async-start(bf16[8,128,128]{2,1,0:T(8,128)(2,1)} %bitcast.25), calls=%async_computation.3 | async-start | bytes 524288 | tf_op jit(solution)/shard_map/all_to_all | solution.py:58
  26.6 1.7 %slice_bitcast_fusion.3 = (bf16[1,128,2048]{2,1,0:T(8,128)(2,1)S(1)}, bf16[1,128,2048]{2,1,0:T(8,128)(2,1)S(1)}, bf16[1,128,2048]{2,1,0:T(8,128)(2,1)S(1)}, bf16[1,128,2048]{2,1,0:T(8,128)(2,1)S(1)}) fusion(bf16[128,8192]{1,0:T(8,128)(2,1)} %param.6), kind=kLoop, calls=%fused_computation.16 | loop fusion | bytes 4194304 | tf_op jit(solution)/shard_map/stack | solution.py:18
  28.3 1.6 %pad_maximum_fusion = bf16[4,128,2048]{2,1,0:T(8,128)(2,1)} fusion(bf16[1,128,2048]{2,1,0:T(8,128)(2,1)S(1)} %get-tuple-element.5, bf16[1,128,2048]{2,1,0:T(8,128)(2,1)S(1)} %get-tuple-element.6, bf16[1,128,2048]{2,1,0:T(8,128)(2,1)S(1)} %get-tuple-element.4, bf16[1,128,2048]{2,1,0:T(8,128)(2,1)S(1)} %get-tuple-element.3), kind=kLoop, calls=%fused_computation.7 | loop fusion | flops 3145728 | bytes 4194304 | tf_op jit(solution)/shard_map/stack | solution.py:18
  29.8 5.3 %all-to-all-done.3 = bf16[8,128,128]{2,1,0:T(8,128)(2,1)S(1)} async-done(((bf16[8,128,128]{2,1,0:T(8,128)(2,1)}), bf16[8,128,128]{2,1,0:T(8,128)(2,1)S(1)}, u32[]{:S(2)}, u32[]{:S(2)}) %all-to-all-start.3) | async-done | bytes 262176 | tf_op jit(solution)/shard_map/all_to_all | solution.py:58
  35.1 4.5 %all-to-all-start.1 = ((bf16[4,128,2048]{2,1,0:T(8,128)(2,1)}), bf16[4,128,2048]{2,1,0:T(8,128)(2,1)}, u32[]{:S(2)}, u32[]{:S(2)}) async-start(bf16[4,128,2048]{2,1,0:T(8,128)(2,1)} %pad_maximum_fusion), calls=%async_computation.1 | async-start | bytes 4194304 | tf_op jit(solution)/shard_map/all_to_all | solution.py:18
  39.6 30.0 %all_gather.3 = bf16[512,640]{1,0:T(8,128)(2,1)S(1)} all-gather(bf16[128,640]{1,0:T(8,128)(2,1)} %param.7), channel_id=1, replica_groups=mesh['rep'=8,'shard'=4] {'shard'}, dimensions={0}, use_global_device_ids=true | all-gather | bytes 819200 | tf_op jit(solution)/shard_map/all_gather | solution.py:16
  69.6 0.0 copy-done
  69.6 3.1 %convolution_convert_fusion = bf16[512,2048]{1,0:T(8,128)(2,1)} fusion(bf16[512,640]{1,0:T(8,128)(2,1)S(1)} %all_gather.3, bf16[2048,640]{1,0:T(8,128)(2,1)S(1)} %copy-done), kind=kOutput, calls=%fused_computation.6 | convolution fusion | flops 1343225856 | bytes 5373952 | tf_op jit(solution)/shard_map/dot_general | solution.py:24
  72.7 0.0 copy-start.3
  72.7 0.0 all-to-all-done.1
  72.7 4.6 %all-to-all-start = ((bf16[4,128,2048]{2,1,0:T(8,128)(2,1)}), bf16[4,128,2048]{2,1,0:T(8,128)(2,1)}, u32[]{:S(2)}, u32[]{:S(2)}) async-start(bf16[4,128,2048]{2,1,0:T(8,128)(2,1)} %bitcast.48), calls=%async_computation | async-start | bytes 4194304 | tf_op jit(solution)/shard_map/all_to_all | solution.py:27
  77.4 0.0 copy-done.3
  77.4 0.6 constant_dynamic-slice_fusion
  78.0 0.6 dynamic_slice.6
  78.6 0.5 broadcast.121
  79.1 2.6 %scatter_custom_fusion = pred[10240]{0:T(1024)(128)(4,1)S(1)} fusion(s32[512]{0:T(512)} %bitcast.55, pred[512]{0:T(512)(128)(4,1)} %broadcast.121, pred[]{:T(512)} %constant.13.clone.1), kind=kCustom, calls=%fused_computation.22 | custom fusion | bytes 10752 | tf_op jit(solution)/shard_map/scatter | solution.py:42
  81.7 0.7 broadcast_subtract_fusion
  82.3 0.6 compare_select_fusion
  82.9 7.0 %scatter_custom_fusion.3 = f32[1920,128]{1,0:T(8,128)} fusion(s32[1024]{0:T(1024)S(1)} %bitcast.59, bf16[1024,128]{1,0:T(8,128)(2,1)S(1)} %bitcast.50, f32[]{:T(128)} %constant.17.clone.1), kind=kCustom, calls=%fused_computation.11 | custom fusion | flops 262144 | bytes 1245188 | tf_op jit(solution)/shard_map/scatter-add | solution.py:12
  89.9 5.7 %fusion.12 = f32[2048,640]{1,0:T(8,128)} fusion(bf16[512,2048]{1,0:T(8,128)(2,1)} %bitcast.8, bf16[512,640]{1,0:T(8,128)(2,1)S(1)} %all_gather.3), kind=kOutput, calls=%fused_computation.38 | convolution fusion | flops 1342177280 | bytes 7995392 | tf_op jit(solution)/shard_map/dot_general | solution.py:21
  95.7 6.5 %reshape.139 = f32[1,10240,128]{2,1,0:T(8,128)} reshape(f32[2048,640]{1,0:T(8,128)} %fusion.12) | data formatting | bytes 10485760 | tf_op jit(solution)/shard_map/reshape | solution.py:44
  102.2 0.9 all-to-all-done
  103.1 0.0 copy-start.1
  103.1 3.3 %copy.17 = bf16[4,16,8,2048]{3,2,0,1:T(8,128)(2,1)} copy(bf16[4,16,8,2048]{3,2,1,0:T(8,128)(2,1)} %bitcast.30) | data formatting | bytes 4194304 | tf_op jit(solution)/shard_map/all_to_all | solution.py:27
  106.4 0.0 copy-done.1
  106.4 8.2 %add_convert_fusion = bf16[1,10240,128]{2,1,0:T(8,128)(2,1)} fusion(f32[1,10240,128]{2,1,0:T(8,128)} %reshape.139, bf16[1,10240,128]{2,1,0:T(8,128)(2,1)S(1)} %copy-done.1, pred[10240]{0:T(1024)(128)(4,1)S(1)} %scatter_custom_fusion), kind=kLoop, calls=%fused_computation.5 | loop fusion | flops 5242880 | bytes 10496000 | tf_op jit(solution)/shard_map/convert_element_type | solution.py:44
  (5 shorter events, 0.0 us)
Async XLA Ops:
  0.6 69.0 %copy-start = (bf16[2048,640]{1,0:T(8,128)(2,1)S(1)}, bf16[2048,640]{1,0:T(8,128)(2,1)}, u32[]{:S(2)}) copy-start(bf16[2048,640]{1,0:T(8,128)(2,1)} %param.8) | copy-start | bytes 7864324
  6.5 14.1 %all-to-all-start.2 = ((s32[8,128,1]{1,2,0:T(1,128)}), s32[8,128,1]{1,2,0:T(1,128)S(1)}, u32[]{:S(2)}, u32[]{:S(2)}) async-start(s32[8,128,1]{1,2,0:T(1,128)} %bitcast.16), calls=%async_computation.2 | async-start | bytes 8192 | tf_op jit(solution)/shard_map/all_to_all | solution.py:59
  14.5 0.6 copy-start.2
  20.6 14.5 %all-to-all-start.3 = ((bf16[8,128,128]{2,1,0:T(8,128)(2,1)}), bf16[8,128,128]{2,1,0:T(8,128)(2,1)S(1)}, u32[]{:S(2)}, u32[]{:S(2)}) async-start(bf16[8,128,128]{2,1,0:T(8,128)(2,1)} %bitcast.25), calls=%async_computation.3 | async-start | bytes 524288 | tf_op jit(solution)/shard_map/all_to_all | solution.py:58
  35.1 37.6 %all-to-all-start.1 = ((bf16[4,128,2048]{2,1,0:T(8,128)(2,1)}), bf16[4,128,2048]{2,1,0:T(8,128)(2,1)}, u32[]{:S(2)}, u32[]{:S(2)}) async-start(bf16[4,128,2048]{2,1,0:T(8,128)(2,1)} %pad_maximum_fusion), calls=%async_computation.1 | async-start | bytes 4194304 | tf_op jit(solution)/shard_map/all_to_all | solution.py:18
  72.7 4.6 %copy-start.3 = (s32[1,8]{1,0:T(1,128)S(1)}, s32[1,8]{1,0:T(1,128)}, u32[]{:S(2)}) copy-start(s32[1,8]{1,0:T(1,128)} %param.11) | copy-start | bytes 100
  72.7 30.3 %all-to-all-start = ((bf16[4,128,2048]{2,1,0:T(8,128)(2,1)}), bf16[4,128,2048]{2,1,0:T(8,128)(2,1)}, u32[]{:S(2)}, u32[]{:S(2)}) async-start(bf16[4,128,2048]{2,1,0:T(8,128)(2,1)} %bitcast.48), calls=%async_computation | async-start | bytes 4194304 | tf_op jit(solution)/shard_map/all_to_all | solution.py:27
  103.1 3.3 %copy-start.1 = (bf16[1,10240,128]{2,1,0:T(8,128)(2,1)S(1)}, bf16[1,10240,128]{2,1,0:T(8,128)(2,1)}, u32[]{:S(2)}) copy-start(bf16[1,10240,128]{2,1,0:T(8,128)(2,1)} %param.9) | copy-start | bytes 7864324
